TPU v7x, 32 devices: a whole 2x2x4 slice. The times are simulated.
32 devices in a mesh: row: 4 (over y, core), col: 8 (over z, x).
Axes of the slice: x: 2, y: 2, z: 4, core: 2. Of those that a mesh axis runs over, the one named last changes fastest.
Arguments:
- first_acts: bfloat16 [2048, 18944], P('col', 'row'), may hold values from -320 to 320, as said below
- second_acts: bfloat16 [2048, 18944], P('row', 'col'), may hold values from -320 to 320, as said below
Outputs:
- row_potential: float32 [18944], P('row')
- column_potential: float32 [18944], P('col')
Inputs may be any that keep to these rules, and one draw needn't show every extreme that they name: `first_acts`: real-valued activations. `second_acts`: real-valued activations.
All inputs are finite; a program needn't handle non-finite values.
Results may differ from a plain program's by a relative error of at most 0.0003.
Values may be sent and summed in bfloat16 or wider, within the bound.
A program may use at most 128 MiB of HBM per device.

v0:
```python
import math
import jax
import jax.numpy as jnp
from jax import lax
from jax.sharding import PartitionSpec as P

NEUR = 18944
SAMP = 2048
ITERS = 4
entropy_scale = 0.004


def row_lse(scores, log_share):
    highest = jnp.max(scores, 1)
    totals = jnp.sum(jnp.exp(scores - highest[:, None]), 1)
    members = lax.axis_size("col")
    maxima, sums = (
        lax.all_to_all(
            highest.reshape(members, -1), "col", split_axis=0, concat_axis=0, tiled=True
        ),
        lax.all_to_all(totals.reshape(members, -1), "col", split_axis=0, concat_axis=0, tiled=True),
    )
    overall = jnp.max(maxima, 0)
    merged_sum = jnp.sum(sums * jnp.exp(maxima - overall[None, :]), 0)
    own_part = log_share - (overall + jnp.log(merged_sum))
    return lax.all_gather(own_part, "col", axis=0, tiled=True)


def col_lse(scores, log_share):
    highest = jnp.max(scores, 0)
    totals = jnp.sum(jnp.exp(scores - highest[None, :]), 0)
    members = lax.axis_size("row")
    maxima, sums = (
        lax.all_to_all(
            highest.reshape(members, -1), "row", split_axis=0, concat_axis=0, tiled=True
        ),
        lax.all_to_all(totals.reshape(members, -1), "row", split_axis=0, concat_axis=0, tiled=True),
    )
    overall = jnp.max(maxima, 0)
    merged_sum = jnp.sum(sums * jnp.exp(maxima - overall[None, :]), 0)
    own_part = log_share - (overall + jnp.log(merged_sum))
    return lax.all_gather(own_part, "row", axis=0, tiled=True)


def shards(first_acts, second_acts):
    full_second = lax.all_gather(second_acts, "row", axis=0, tiled=True)
    rows_here = first_acts.shape[1]
    cols_here = second_acts.shape[1]
    segment = lax.all_gather(first_acts, "col", axis=0, tiled=True)
    products = lax.dot_general(
        segment, full_second, (((0,), (0,)), ((), ())), preferred_element_type=jnp.float32
    )
    widened = segment.astype(jnp.float32)
    products, first_squares = (products, jnp.sum(widened * widened, 0))
    second_wide = full_second.astype(jnp.float32)
    second_squares = jnp.sum(second_wide * second_wide, 0)
    inv_first = 1.0 / jnp.sqrt(first_squares / SAMP + 1e-06)
    inv_second = 1.0 / jnp.sqrt(second_squares / SAMP + 1e-06)
    logk = products * inv_first[:, None] * inv_second[None, :] * (1.0 / (SAMP * entropy_scale))
    log_share = -math.log(NEUR)
    row_potential = jnp.zeros((rows_here,), jnp.float32)
    column_potential = jnp.zeros((cols_here,), jnp.float32)
    for step in range(ITERS):
        row_potential = row_lse(column_potential[None, :] + logk, log_share)
        column_potential = col_lse(row_potential[:, None] + logk, log_share)
    return (row_potential, column_potential)


def solution(mesh):
    return jax.shard_map(
        shards,
        mesh=mesh,
        in_specs=(P("col", "row"), P("row", "col")),
        out_specs=(P("row"), P("col")),
        check_vma=False,
    )
```

profile of v0, /device:TPU:0, one launch (start us, length us, event | category | flops | bytes accessed | tf_op | source)
XLA Modules:
  0.0 1064.9 jit_solution(205873519118053908)
XLA Ops:
  8.6 69.4 %all-gather.5.cloned.1.call-done = bf16[2048,2368]{0,1:T(8,128)(2,1)} async-done(((bf16[512,2368]{0,1:T(8,128)(2,1)}), bf16[2048,2368]{0,1:T(8,128)(2,1)}) %all-gather.5.cloned.1.call-update) | async-done | bytes 9699344 | tf_op jit(solution)/shard_map/all_gather | solution.py:46
  78.0 5.7 multiply_reduce_fusion.1
  83.7 368.1 %all-gather.3.cloned.1.call-done = bf16[2048,4736]{1,0:T(8,128)(2,1)} async-done(((bf16[256,4736]{1,0:T(8,128)(2,1)}), bf16[2048,4736]{1,0:T(8,128)(2,1)}) %all-gather.3.cloned.1.call-update) | async-done | bytes 19398672 | tf_op jit(solution)/shard_map/all_gather | solution.py:49
  451.8 8.4 multiply_reduce_fusion
  460.2 59.7 %fusion.24 = (f32[4736]{0:T(1024)S(1)}, f32[4736,2368]{0,1:T(8,128)}) fusion(f32[2368]{0:T(1024)S(1)} %add_rsqrt_fusion.1, f32[4736]{0:T(1024)S(1)} %add_rsqrt_fusion, bf16[2048,2368]{0,1:T(8,128)(2,1)} %all-gather.5.cloned.1.call-done, bf16[2048,4736]{1,0:T(8,128)(2,1)} %all-gather.3.cloned.1.call-done), kind=kOutput, calls=%fused_computation.60 | convolution fusion | flops 45980872704 | bytes 74004736 | tf_op jit(solution)/shard_map/dot_general | solution.py:50
  520.6 4.6 all-to-all-start
  525.2 17.3 %exponential_reduce_fusion.7 = f32[4736]{0:T(1024)S(1)} fusion(f32[4736,2368]{0,1:T(8,128)} %get-tuple-element.3, f32[4736]{0:T(1024)S(1)} %get-tuple-element.2), kind=kLoop, calls=%fused_computation.7 | loop fusion | flops 22424960 | bytes 44897280 | tf_op jit(solution)/shard_map/reduce_sum | solution.py:15
  543.3 6.0 all-to-all-start.1
  550.5 5.3 all-to-all-done.1
  556.0 33.5 %all-reduce = f32[4736]{0:T(1024)S(1)} all-reduce(f32[4736]{0:T(1024)S(1)} %subtract_dynamic-update-slice_fusion.7), channel_id=1, replica_groups=mesh['row'=4,'col'=8] {'col'}, use_global_device_ids=true, to_apply=%add | all-reduce | flops 4736 | bytes 37888
  589.5 14.8 %add_reduce_fusion.6 = f32[2368]{0:T(1024)S(1)} fusion(f32[4736,2368]{0,1:T(8,128)} %get-tuple-element.3, f32[4736]{0:T(1024)S(1)} %all-reduce), kind=kLoop, calls=%fused_computation.15 | loop fusion | flops 22427328 | bytes 44887808 | tf_op jit(solution)/shard_map/reduce_max | solution.py:30
  605.0 3.3 all-to-all-start.2
  608.2 15.9 %exponential_reduce_fusion.6 = f32[2368]{0:T(1024)S(1)} fusion(f32[4736,2368]{0,1:T(8,128)} %get-tuple-element.3, f32[2368]{0:T(1024)S(1)} %add_reduce_fusion.6, f32[4736]{0:T(1024)S(1)} %all-reduce), kind=kLoop, calls=%fused_computation.6 | loop fusion | flops 33642176 | bytes 44897280 | tf_op jit(solution)/shard_map/reduce_sum | solution.py:31
  624.8 3.3 all-to-all-start.3
  632.0 10.1 all-reduce.1
  642.1 16.4 %add_reduce_fusion.5 = f32[4736]{0:T(1024)S(1)} fusion(f32[4736,2368]{0,1:T(8,128)} %get-tuple-element.3, f32[2368]{0:T(1024)S(1)} %all-reduce.1), kind=kLoop, calls=%fused_computation.14 | loop fusion | flops 22424960 | bytes 44887808 | tf_op jit(solution)/shard_map/reduce_max | solution.py:14
  659.3 3.3 all-to-all-start.4
  662.6 18.4 %exponential_reduce_fusion.5 = f32[4736]{0:T(1024)S(1)} fusion(f32[4736,2368]{0,1:T(8,128)} %get-tuple-element.3, f32[4736]{0:T(1024)S(1)} %add_reduce_fusion.5, f32[2368]{0:T(1024)S(1)} %all-reduce.1), kind=kLoop, calls=%fused_computation.5 | loop fusion | flops 33639808 | bytes 44906752 | tf_op jit(solution)/shard_map/reduce_sum | solution.py:15
  681.7 5.9 all-to-all-start.5
  687.7 6.6 all-to-all-done.5
  694.4 33.5 %all-reduce.2 = f32[4736]{0:T(1024)S(1)} all-reduce(f32[4736]{0:T(1024)S(1)} %subtract_dynamic-update-slice_fusion.5), channel_id=1, replica_groups=mesh['row'=4,'col'=8] {'col'}, use_global_device_ids=true, to_apply=%add.2 | all-reduce | flops 4736 | bytes 37888
  727.9 14.8 %add_reduce_fusion.4 = f32[2368]{0:T(1024)S(1)} fusion(f32[4736,2368]{0,1:T(8,128)} %get-tuple-element.3, f32[4736]{0:T(1024)S(1)} %all-reduce.2), kind=kLoop, calls=%fused_computation.13 | loop fusion | flops 22427328 | bytes 44887808 | tf_op jit(solution)/shard_map/reduce_max | solution.py:30
  746.6 15.9 %exponential_reduce_fusion.4 = f32[2368]{0:T(1024)S(1)} fusion(f32[4736,2368]{0,1:T(8,128)} %get-tuple-element.3, f32[2368]{0:T(1024)S(1)} %add_reduce_fusion.4, f32[4736]{0:T(1024)S(1)} %all-reduce.2), kind=kLoop, calls=%fused_computation.4 | loop fusion | flops 33642176 | bytes 44897280 | tf_op jit(solution)/shard_map/reduce_sum | solution.py:31
  763.1 3.3 all-to-all-start.7
  766.4 3.8 all-to-all-done.7
  770.4 10.1 all-reduce.3
  780.5 16.4 %add_reduce_fusion.3 = f32[4736]{0:T(1024)S(1)} fusion(f32[4736,2368]{0,1:T(8,128)} %get-tuple-element.3, f32[2368]{0:T(1024)S(1)} %all-reduce.3), kind=kLoop, calls=%fused_computation.12 | loop fusion | flops 22424960 | bytes 44887808 | tf_op jit(solution)/shard_map/reduce_max | solution.py:14
  797.6 3.3 all-to-all-start.8
  801.0 18.4 %exponential_reduce_fusion.3 = f32[4736]{0:T(1024)S(1)} fusion(f32[4736,2368]{0,1:T(8,128)} %get-tuple-element.3, f32[4736]{0:T(1024)S(1)} %add_reduce_fusion.3, f32[2368]{0:T(1024)S(1)} %all-reduce.3), kind=kLoop, calls=%fused_computation.3 | loop fusion | flops 33639808 | bytes 44906752 | tf_op jit(solution)/shard_map/reduce_sum | solution.py:15
  820.1 5.9 all-to-all-start.9
  826.0 6.6 all-to-all-done.9
  832.8 33.5 %all-reduce.4 = f32[4736]{0:T(1024)S(1)} all-reduce(f32[4736]{0:T(1024)S(1)} %subtract_dynamic-update-slice_fusion.3), channel_id=1, replica_groups=mesh['row'=4,'col'=8] {'col'}, use_global_device_ids=true, to_apply=%add.4 | all-reduce | flops 4736 | bytes 37888
  866.2 14.8 %add_reduce_fusion.2 = f32[2368]{0:T(1024)S(1)} fusion(f32[4736,2368]{0,1:T(8,128)} %get-tuple-element.3, f32[4736]{0:T(1024)S(1)} %all-reduce.4), kind=kLoop, calls=%fused_computation.11 | loop fusion | flops 22427328 | bytes 44887808 | tf_op jit(solution)/shard_map/reduce_max | solution.py:30
  881.7 3.5 all-to-all-start.10
  885.2 15.9 %exponential_reduce_fusion.2 = f32[2368]{0:T(1024)S(1)} fusion(f32[4736,2368]{0,1:T(8,128)} %get-tuple-element.3, f32[2368]{0:T(1024)S(1)} %add_reduce_fusion.2, f32[4736]{0:T(1024)S(1)} %all-reduce.4), kind=kLoop, calls=%fused_computation.2 | loop fusion | flops 33642176 | bytes 44897280 | tf_op jit(solution)/shard_map/reduce_sum | solution.py:31
  901.7 3.3 all-to-all-start.11
  905.0 3.8 all-to-all-done.11
  908.9 10.1 all-reduce.5
  919.0 16.4 %add_reduce_fusion.1 = f32[4736]{0:T(1024)S(1)} fusion(f32[4736,2368]{0,1:T(8,128)} %get-tuple-element.3, f32[2368]{0:T(1024)S(1)} %all-reduce.5), kind=kLoop, calls=%fused_computation.10 | loop fusion | flops 22424960 | bytes 44887808 | tf_op jit(solution)/shard_map/reduce_max | solution.py:14
  936.2 3.3 all-to-all-start.12
  939.5 18.4 %exponential_reduce_fusion.1 = f32[4736]{0:T(1024)S(1)} fusion(f32[4736,2368]{0,1:T(8,128)} %get-tuple-element.3, f32[4736]{0:T(1024)S(1)} %add_reduce_fusion.1, f32[2368]{0:T(1024)S(1)} %all-reduce.5), kind=kLoop, calls=%fused_computation.1 | loop fusion | flops 33639808 | bytes 44906752 | tf_op jit(solution)/shard_map/reduce_sum | solution.py:15
  958.6 5.9 all-to-all-start.13
  964.6 6.6 all-to-all-done.13
  971.3 33.5 %all-reduce.6 = f32[4736]{0:T(1024)S(1)} all-reduce(f32[4736]{0:T(1024)S(1)} %subtract_dynamic-update-slice_fusion.1), channel_id=1, replica_groups=mesh['row'=4,'col'=8] {'col'}, use_global_device_ids=true, to_apply=%add.6 | all-reduce | flops 4736 | bytes 37888
  1004.8 14.8 %add_reduce_fusion = f32[2368]{0:T(1024)S(1)} fusion(f32[4736,2368]{0,1:T(8,128)} %get-tuple-element.3, f32[4736]{0:T(1024)S(1)} %all-reduce.6), kind=kLoop, calls=%fused_computation.9 | loop fusion | flops 22427328 | bytes 44887808 | tf_op jit(solution)/shard_map/reduce_max | solution.py:30
  1023.5 15.9 %exponential_reduce_fusion = f32[2368]{0:T(1024)S(1)} fusion(f32[4736,2368]{0,1:T(8,128)} %get-tuple-element.3, f32[2368]{0:T(1024)S(1)} %add_reduce_fusion, f32[4736]{0:T(1024)S(1)} %all-reduce.6), kind=kLoop, calls=%fused_computation | loop fusion | flops 33642176 | bytes 44897280 | tf_op jit(solution)/shard_map/reduce_sum | solution.py:31
  1043.4 3.8 all-to-all-done.15
  1047.3 10.7 %all-reduce.7 = f32[2368]{0:T(1024)} all-reduce(f32[2368]{0:T(1024)S(1)} %subtract_dynamic-update-slice_fusion), channel_id=1, replica_groups=mesh['row'=4,'col'=8] {'row'}, use_global_device_ids=true, to_apply=%add.7 | all-reduce | flops 2368 | bytes 18944
  (74 shorter events, 27.4 us)
Async XLA Ops:
  7.2 70.8 %all-gather.5.cloned.1.call-start = ((), (), s32[]{:S(2)}) async-start(), calls=%async_computation.17 | async-start | bytes 12124160 | tf_op jit(solution)/shard_map/all_gather | solution.py:46
  7.9 443.9 %all-gather.3.cloned.1.call-start = ((), (), s32[]{:S(2)}) async-start(), calls=%async_computation.16 | async-start | bytes 21823488 | tf_op jit(solution)/shard_map/all_gather | solution.py:49
  519.9 29.3 %copy-start.2 = (u32[32]{0:T(128)S(1)}, u32[32]{0:T(128)}, u32[]{:S(2)}) copy-start(u32[32]{0:T(128)} %constant.20) | copy-start | bytes 388
  520.6 22.6 %all-to-all-start = ((f32[8,1,592]{2,1,0:T(1,128)}), f32[8,1,592]{2,1,0:T(1,128)S(1)}, u32[]{:S(2)}, u32[]{:S(2)}) async-start(f32[8,1,592]{2,1,0:T(1,128)} %all_to_all.128), calls=%async_computation | async-start | bytes 40960 | tf_op jit(solution)/shard_map/all_to_all | solution.py:18
  543.3 12.6 %all-to-all-start.1 = ((f32[8,1,592]{2,1,0:T(1,128)}), f32[8,1,592]{2,1,0:T(1,128)S(1)}, u32[]{:S(2)}, u32[]{:S(2)}) async-start(f32[8,1,592]{2,1,0:T(1,128)} %all_to_all.130), calls=%async_computation.1 | async-start | bytes 40960 | tf_op jit(solution)/shard_map/all_to_all | solution.py:21
  589.5 38.5 %copy-start.1 = (u32[32]{0:T(128)S(1)}, u32[32]{0:T(128)}, u32[]{:S(2)}) copy-start(u32[32]{0:T(128)} %constant.25) | copy-start | bytes 388
  605.0 19.8 %all-to-all-start.2 = ((f32[4,1,592]{2,1,0:T(1,128)}), f32[4,1,592]{2,1,0:T(1,128)S(1)}, u32[]{:S(2)}, u32[]{:S(2)}) async-start(f32[4,1,592]{2,1,0:T(1,128)} %all_to_all.134), calls=%async_computation.2 | async-start | bytes 20480 | tf_op jit(solution)/shard_map/all_to_all | solution.py:34
  624.8 7.1 all-to-all-start.3
  659.3 22.5 %all-to-all-start.4 = ((f32[8,1,592]{2,1,0:T(1,128)}), f32[8,1,592]{2,1,0:T(1,128)S(1)}, u32[]{:S(2)}, u32[]{:S(2)}) async-start(f32[8,1,592]{2,1,0:T(1,128)} %all_to_all.140), calls=%async_computation.4 | async-start | bytes 40960 | tf_op jit(solution)/shard_map/all_to_all | solution.py:18
  681.7 12.5 %all-to-all-start.5 = ((f32[8,1,592]{2,1,0:T(1,128)}), f32[8,1,592]{2,1,0:T(1,128)S(1)}, u32[]{:S(2)}, u32[]{:S(2)}) async-start(f32[8,1,592]{2,1,0:T(1,128)} %all_to_all.142), calls=%async_computation.5 | async-start | bytes 40960 | tf_op jit(solution)/shard_map/all_to_all | solution.py:21
  743.3 19.8 %all-to-all-start.6 = ((f32[4,1,592]{2,1,0:T(1,128)}), f32[4,1,592]{2,1,0:T(1,128)S(1)}, u32[]{:S(2)}, u32[]{:S(2)}) async-start(f32[4,1,592]{2,1,0:T(1,128)} %all_to_all.146), calls=%async_computation.6 | async-start | bytes 20480 | tf_op jit(solution)/shard_map/all_to_all | solution.py:34
  763.1 7.1 all-to-all-start.7
  797.6 22.5 %all-to-all-start.8 = ((f32[8,1,592]{2,1,0:T(1,128)}), f32[8,1,592]{2,1,0:T(1,128)S(1)}, u32[]{:S(2)}, u32[]{:S(2)}) async-start(f32[8,1,592]{2,1,0:T(1,128)} %all_to_all.152), calls=%async_computation.8 | async-start | bytes 40960 | tf_op jit(solution)/shard_map/all_to_all | solution.py:18
  820.1 12.5 %all-to-all-start.9 = ((f32[8,1,592]{2,1,0:T(1,128)}), f32[8,1,592]{2,1,0:T(1,128)S(1)}, u32[]{:S(2)}, u32[]{:S(2)}) async-start(f32[8,1,592]{2,1,0:T(1,128)} %all_to_all.154), calls=%async_computation.9 | async-start | bytes 40960 | tf_op jit(solution)/shard_map/all_to_all | solution.py:21
  881.7 20.0 %all-to-all-start.10 = ((f32[4,1,592]{2,1,0:T(1,128)}), f32[4,1,592]{2,1,0:T(1,128)S(1)}, u32[]{:S(2)}, u32[]{:S(2)}) async-start(f32[4,1,592]{2,1,0:T(1,128)} %all_to_all.158), calls=%async_computation.10 | async-start | bytes 20480 | tf_op jit(solution)/shard_map/all_to_all | solution.py:34
  901.7 7.0 all-to-all-start.11
  936.2 22.5 %all-to-all-start.12 = ((f32[8,1,592]{2,1,0:T(1,128)}), f32[8,1,592]{2,1,0:T(1,128)S(1)}, u32[]{:S(2)}, u32[]{:S(2)}) async-start(f32[8,1,592]{2,1,0:T(1,128)} %all_to_all.164), calls=%async_computation.12 | async-start | bytes 40960 | tf_op jit(solution)/shard_map/all_to_all | solution.py:18
  958.6 12.5 %all-to-all-start.13 = ((f32[8,1,592]{2,1,0:T(1,128)}), f32[8,1,592]{2,1,0:T(1,128)S(1)}, u32[]{:S(2)}, u32[]{:S(2)}) async-start(f32[8,1,592]{2,1,0:T(1,128)} %all_to_all.166), calls=%async_computation.13 | async-start | bytes 40960 | tf_op jit(solution)/shard_map/all_to_all | solution.py:21
  1004.8 34.6 %copy-start = (f32[4736]{0:T(1024)}, f32[4736]{0:T(1024)S(1)}, u32[]{:S(2)}) copy-start(f32[4736]{0:T(1024)S(1)} %all-reduce.6) | copy-start | bytes 56836
  1020.3 19.8 %all-to-all-start.14 = ((f32[4,1,592]{2,1,0:T(1,128)}), f32[4,1,592]{2,1,0:T(1,128)S(1)}, u32[]{:S(2)}, u32[]{:S(2)}) async-start(f32[4,1,592]{2,1,0:T(1,128)} %all_to_all.170), calls=%async_computation.14 | async-start | bytes 20480 | tf_op jit(solution)/shard_map/all_to_all | solution.py:34
  1040.1 7.1 all-to-all-start.15
Sparse Core Ops, SparseCore 0:
  9.5 68.4 all-gather.4
  79.5 372.2 all-gather.2
where the time goes:
time: 1070 us; the launch traced here: 1060 us
  waiting for transfers between devices  478 us (45%)
  other arithmetic  260 us (24%)
  blocking collectives  175 us (16%)
  starting transfers between devices  64.7 us (6%)
  matrix products  59.7 us (6%)
  between operations  15.7 us (1%)
  local copies, waits for them, and re-layouts  12.3 us (1%)
    all_gather x1, waiting for transfers between devices, shards(): segment = lax.all_gather(first_acts, 'col', axis=0, tiled=True)  368 us
    unnamed x8, blocking collectives  175 us
    reduce_sum x4, other arithmetic, row_lse(): totals = jnp.sum(jnp.exp(scores - highest[:, None]), 1)  72.5 us
    all_gather x1, waiting for transfers between devices, shards(): full_second = lax.all_gather(second_acts, 'row', axis=0, tiled=True)  69.4 us
    reduce_sum x4, other arithmetic, col_lse(): totals = jnp.sum(jnp.exp(scores - highest[None, :]), 0)  63.5 us
    dot_general x1, matrix products, shards(): lax.dot_general(segment, full_second, (((0,), (0,)), ((), ())), preferred...  59.7 us
    reduce_max x4, other arithmetic, col_lse(): highest = jnp.max(scores, 0)  59.1 us
    reduce_max x3, other arithmetic, row_lse(): highest = jnp.max(scores, 1)  49.3 us
  transfers between devices with their start and end apart: 18, of which 10 were waited for; matrix products, arithmetic and copies ran while one was open for 13% of the time, Pallas kernels for 0%

commit v1 on v0

--- a/solution.py
+++ b/solution.py
@@ -43,7 +43,15 @@
 
 
 def shards(first_acts, second_acts):
-    full_second = lax.all_gather(second_acts, "row", axis=0, tiled=True)
+    devices = lax.axis_size("row")
+    held, blocks = (second_acts, [second_acts])
+    for _ in range(devices - 1):
+        held = lax.ppermute(held, "row", [(i, (i + 1) % devices) for i in range(devices)])
+        blocks.insert(0, held)
+    row_of_blocks = jnp.concatenate(blocks, axis=0)
+    full_second = jnp.roll(
+        row_of_blocks, (lax.axis_index("row") + 1) * second_acts.shape[0], axis=0
+    )
     rows_here = first_acts.shape[1]
     cols_here = second_acts.shape[1]
     segment = lax.all_gather(first_acts, "col", axis=0, tiled=True)

time: 1070 us -> 1000 us (0.935)
  waiting for transfers between devices: 478 us -> 386 us
  local copies, waits for them, and re-layouts: 12.3 us -> 35.7 us
    all_gather x1, waiting for transfers between devices: 368 us -> 259 us  [shards(): segment = lax.all_gather(first_acts, 'col', axis=0, tiled=True)]
    ppermute x0 -> x3, waiting for transfers between devices: none -> 87.7 us  [shards(): lax.ppermute(held, 'row', [(i, (i + 1) % devices) for i in range(devices)])]
    all_gather x1 -> x0, waiting for transfers between devices: 69.4 us -> none  [shards(): full_second = lax.all_gather(second_acts, 'row', axis=0, tiled=True)]
    unnamed x16 -> x23, local copies, waits for them, and re-layouts: 1.21 us -> 21.3 us
  transfers between devices with their start and end apart: 18 -> 20, of which waited for: 10 -> 12; matrix products, arithmetic and copies ran while one was open for 13% -> 17% of each run, Pallas kernels for 0% -> 0%
where the time goes in v1:
time: 1000 us; the launch traced here: 998 us
  waiting for transfers between devices  386 us (39%)
  other arithmetic  260 us (26%)
  blocking collectives  175 us (18%)
  starting transfers between devices  65.2 us (7%)
  matrix products  59.8 us (6%)
  local copies, waits for them, and re-layouts  35.7 us (4%)
  between operations  15.7 us (2%)
    all_gather x1, waiting for transfers between devices, shards(): segment = lax.all_gather(first_acts, 'col', axis=0, tiled=True)  259 us
    unnamed x8, blocking collectives  175 us
    ppermute x3, waiting for transfers between devices, shards(): lax.ppermute(held, 'row', [(i, (i + 1) % devices) for i in range(devices)])  87.7 us
    reduce_sum x4, other arithmetic, row_lse(): totals = jnp.sum(jnp.exp(scores - highest[:, None]), 1)  72.5 us
    reduce_sum x4, other arithmetic, col_lse(): totals = jnp.sum(jnp.exp(scores - highest[None, :]), 0)  63.5 us
    dot_general x1, matrix products, shards(): lax.dot_general(segment, full_second, (((0,), (0,)), ((), ())), preferred...  59.8 us
    reduce_max x4, other arithmetic, col_lse(): highest = jnp.max(scores, 0)  59.1 us
    reduce_max x3, other arithmetic, row_lse(): highest = jnp.max(scores, 1)  49.3 us
  transfers between devices with their start and end apart: 20, of which 12 were waited for; matrix products, arithmetic and copies ran while one was open for 17% of the time, Pallas kernels for 0%

profile of v1, /device:TPU:0, one launch (start us, length us, event | category | flops | bytes accessed | tf_op | source)
XLA Modules:
  0.0 997.6 jit_solution(18200518527465197740)
XLA Ops:
  8.4 29.4 %collective-permute-done = bf16[512,2368]{0,1:T(8,128)(2,1)S(1)} collective-permute-done((bf16[512,2368]{0,1:T(8,128)(2,1)}, bf16[512,2368]{0,1:T(8,128)(2,1)S(1)}, u32[]{:S(2)}, u32[]{:S(2)}) %collective-permute-start) | collective-permute-done | bytes 2424864 | tf_op jit(solution)/shard_map/ppermute | solution.py:49
  37.9 29.0 %collective-permute-done.1 = bf16[512,2368]{0,1:T(8,128)(2,1)} collective-permute-done((bf16[512,2368]{0,1:T(8,128)(2,1)S(1)}, bf16[512,2368]{0,1:T(8,128)(2,1)}, u32[]{:S(2)}, u32[]{:S(2)}) %collective-permute-start.1) | collective-permute-done | bytes 2424864 | tf_op jit(solution)/shard_map/ppermute | solution.py:49
  66.9 29.3 %collective-permute-done.2 = bf16[512,2368]{0,1:T(8,128)(2,1)} collective-permute-done((bf16[512,2368]{0,1:T(8,128)(2,1)}, bf16[512,2368]{0,1:T(8,128)(2,1)}, u32[]{:S(2)}, u32[]{:S(2)}) %collective-permute-start.2) | collective-permute-done | bytes 2424864 | tf_op jit(solution)/shard_map/ppermute | solution.py:49
  96.2 3.4 constant_dynamic-update-slice_fusion.7
  107.9 3.4 constant_dynamic-update-slice_fusion.3
  116.2 3.3 constant_dynamic-update-slice_fusion
  119.6 5.9 multiply_reduce_fusion.1
  125.4 259.0 %all-gather.2.cloned.1.call-done = bf16[2048,4736]{1,0:T(8,128)(2,1)} async-done(((bf16[256,4736]{1,0:T(8,128)(2,1)}), bf16[2048,4736]{1,0:T(8,128)(2,1)}) %all-gather.2.cloned.1.call-update) | async-done | bytes 19398672 | tf_op jit(solution)/shard_map/all_gather | solution.py:57
  384.5 8.4 multiply_reduce_fusion
  392.9 59.8 %fusion.26 = (f32[4736]{0:T(1024)S(1)}, f32[2368,4736]{1,0:T(8,128)}) fusion(f32[2368]{0:T(1024)S(1)} %add_rsqrt_fusion.1, f32[4736]{0:T(1024)S(1)} %add_rsqrt_fusion, bf16[2048,4736]{1,0:T(8,128)(2,1)} %all-gather.2.cloned.1.call-done, bf16[4096,2368]{0,1:T(8,128)(2,1)} %constant_dynamic-update-slice_fusion, s32[]{:T(128)S(6)} %select_n.14), kind=kOutput, calls=%fused_computation.70 | convolution fusion | flops 45980872704 | bytes 74004736 | tf_op jit(solution)/shard_map/dot_general | solution.py:58
  453.3 4.6 all-to-all-start
  457.9 17.3 %exponential_reduce_fusion.7 = f32[4736]{0:T(1024)S(1)} fusion(f32[2368,4736]{1,0:T(8,128)} %get-tuple-element.3, f32[4736]{0:T(1024)S(1)} %get-tuple-element.2), kind=kLoop, calls=%fused_computation.7 | loop fusion | flops 22424960 | bytes 44897280 | tf_op jit(solution)/shard_map/reduce_sum | solution.py:15
  476.0 6.0 all-to-all-start.1
  483.2 5.3 all-to-all-done.1
  488.7 33.5 %all-reduce = f32[4736]{0:T(1024)S(1)} all-reduce(f32[4736]{0:T(1024)S(1)} %subtract_dynamic-update-slice_fusion.7), channel_id=1, replica_groups=mesh['row'=4,'col'=8] {'col'}, use_global_device_ids=true, to_apply=%add | all-reduce | flops 4736 | bytes 37888
  522.2 14.8 %add_reduce_fusion.6 = f32[2368]{0:T(1024)S(1)} fusion(f32[2368,4736]{1,0:T(8,128)} %get-tuple-element.3, f32[4736]{0:T(1024)S(1)} %all-reduce), kind=kLoop, calls=%fused_computation.15 | loop fusion | flops 22427328 | bytes 44887808 | tf_op jit(solution)/shard_map/reduce_max | solution.py:30
  537.7 3.5 all-to-all-start.2
  541.1 15.9 %exponential_reduce_fusion.6 = f32[2368]{0:T(1024)S(1)} fusion(f32[2368,4736]{1,0:T(8,128)} %get-tuple-element.3, f32[2368]{0:T(1024)S(1)} %add_reduce_fusion.6, f32[4736]{0:T(1024)S(1)} %all-reduce), kind=kLoop, calls=%fused_computation.6 | loop fusion | flops 33642176 | bytes 44897280 | tf_op jit(solution)/shard_map/reduce_sum | solution.py:31
  564.9 10.1 %all-reduce.1 = f32[2368]{0:T(1024)S(1)} all-reduce(f32[2368]{0:T(1024)S(1)} %subtract_dynamic-update-slice_fusion.6), channel_id=1, replica_groups=mesh['row'=4,'col'=8] {'row'}, use_global_device_ids=true, to_apply=%add.1 | all-reduce | flops 2368 | bytes 18944
  575.0 16.4 %add_reduce_fusion.5 = f32[4736]{0:T(1024)S(1)} fusion(f32[2368,4736]{1,0:T(8,128)} %get-tuple-element.3, f32[2368]{0:T(1024)S(1)} %all-reduce.1), kind=kLoop, calls=%fused_computation.14 | loop fusion | flops 22424960 | bytes 44887808 | tf_op jit(solution)/shard_map/reduce_max | solution.py:14
  595.5 18.4 %exponential_reduce_fusion.5 = f32[4736]{0:T(1024)S(1)} fusion(f32[2368,4736]{1,0:T(8,128)} %get-tuple-element.3, f32[4736]{0:T(1024)S(1)} %add_reduce_fusion.5, f32[2368]{0:T(1024)S(1)} %all-reduce.1), kind=kLoop, calls=%fused_computation.5 | loop fusion | flops 33639808 | bytes 44906752 | tf_op jit(solution)/shard_map/reduce_sum | solution.py:15
  614.6 5.9 all-to-all-start.5
  620.6 6.6 all-to-all-done.5
  627.3 33.5 %all-reduce.2 = f32[4736]{0:T(1024)S(1)} all-reduce(f32[4736]{0:T(1024)S(1)} %subtract_dynamic-update-slice_fusion.5), channel_id=1, replica_groups=mesh['row'=4,'col'=8] {'col'}, use_global_device_ids=true, to_apply=%add.2 | all-reduce | flops 4736 | bytes 37888
  660.8 14.8 %add_reduce_fusion.4 = f32[2368]{0:T(1024)S(1)} fusion(f32[2368,4736]{1,0:T(8,128)} %get-tuple-element.3, f32[4736]{0:T(1024)S(1)} %all-reduce.2), kind=kLoop, calls=%fused_computation.13 | loop fusion | flops 22427328 | bytes 44887808 | tf_op jit(solution)/shard_map/reduce_max | solution.py:30
  679.5 15.9 %exponential_reduce_fusion.4 = f32[2368]{0:T(1024)S(1)} fusion(f32[2368,4736]{1,0:T(8,128)} %get-tuple-element.3, f32[2368]{0:T(1024)S(1)} %add_reduce_fusion.4, f32[4736]{0:T(1024)S(1)} %all-reduce.2), kind=kLoop, calls=%fused_computation.4 | loop fusion | flops 33642176 | bytes 44897280 | tf_op jit(solution)/shard_map/reduce_sum | solution.py:31
  699.3 3.8 all-to-all-done.7
  703.3 10.1 %all-reduce.3 = f32[2368]{0:T(1024)S(1)} all-reduce(f32[2368]{0:T(1024)S(1)} %subtract_dynamic-update-slice_fusion.4), channel_id=1, replica_groups=mesh['row'=4,'col'=8] {'row'}, use_global_device_ids=true, to_apply=%add.3 | all-reduce | flops 2368 | bytes 18944
  713.4 16.4 %add_reduce_fusion.3 = f32[4736]{0:T(1024)S(1)} fusion(f32[2368,4736]{1,0:T(8,128)} %get-tuple-element.3, f32[2368]{0:T(1024)S(1)} %all-reduce.3), kind=kLoop, calls=%fused_computation.12 | loop fusion | flops 22424960 | bytes 44887808 | tf_op jit(solution)/shard_map/reduce_max | solution.py:14
  730.5 3.3 all-to-all-start.8
  733.9 18.4 %exponential_reduce_fusion.3 = f32[4736]{0:T(1024)S(1)} fusion(f32[2368,4736]{1,0:T(8,128)} %get-tuple-element.3, f32[4736]{0:T(1024)S(1)} %add_reduce_fusion.3, f32[2368]{0:T(1024)S(1)} %all-reduce.3), kind=kLoop, calls=%fused_computation.3 | loop fusion | flops 33639808 | bytes 44906752 | tf_op jit(solution)/shard_map/reduce_sum | solution.py:15
  753.0 5.9 all-to-all-start.9
  758.9 6.6 all-to-all-done.9
  765.7 33.5 %all-reduce.4 = f32[4736]{0:T(1024)S(1)} all-reduce(f32[4736]{0:T(1024)S(1)} %subtract_dynamic-update-slice_fusion.3), channel_id=1, replica_groups=mesh['row'=4,'col'=8] {'col'}, use_global_device_ids=true, to_apply=%add.4 | all-reduce | flops 4736 | bytes 37888
  799.1 14.8 %add_reduce_fusion.2 = f32[2368]{0:T(1024)S(1)} fusion(f32[2368,4736]{1,0:T(8,128)} %get-tuple-element.3, f32[4736]{0:T(1024)S(1)} %all-reduce.4), kind=kLoop, calls=%fused_computation.11 | loop fusion | flops 22427328 | bytes 44887808 | tf_op jit(solution)/shard_map/reduce_max | solution.py:30
  817.8 15.9 %exponential_reduce_fusion.2 = f32[2368]{0:T(1024)S(1)} fusion(f32[2368,4736]{1,0:T(8,128)} %get-tuple-element.3, f32[2368]{0:T(1024)S(1)} %add_reduce_fusion.2, f32[4736]{0:T(1024)S(1)} %all-reduce.4), kind=kLoop, calls=%fused_computation.2 | loop fusion | flops 33642176 | bytes 44897280 | tf_op jit(solution)/shard_map/reduce_sum | solution.py:31
  837.7 3.8 all-to-all-done.11
  841.6 10.1 %all-reduce.5 = f32[2368]{0:T(1024)S(1)} all-reduce(f32[2368]{0:T(1024)S(1)} %subtract_dynamic-update-slice_fusion.2), channel_id=1, replica_groups=mesh['row'=4,'col'=8] {'row'}, use_global_device_ids=true, to_apply=%add.5 | all-reduce | flops 2368 | bytes 18944
  851.7 16.4 %add_reduce_fusion.1 = f32[4736]{0:T(1024)S(1)} fusion(f32[2368,4736]{1,0:T(8,128)} %get-tuple-element.3, f32[2368]{0:T(1024)S(1)} %all-reduce.5), kind=kLoop, calls=%fused_computation.10 | loop fusion | flops 22424960 | bytes 44887808 | tf_op jit(solution)/shard_map/reduce_max | solution.py:14
  868.9 3.6 all-to-all-start.12
  872.5 18.4 %exponential_reduce_fusion.1 = f32[4736]{0:T(1024)S(1)} fusion(f32[2368,4736]{1,0:T(8,128)} %get-tuple-element.3, f32[4736]{0:T(1024)S(1)} %add_reduce_fusion.1, f32[2368]{0:T(1024)S(1)} %all-reduce.5), kind=kLoop, calls=%fused_computation.1 | loop fusion | flops 33639808 | bytes 44906752 | tf_op jit(solution)/shard_map/reduce_sum | solution.py:15
  891.6 5.7 all-to-all-start.13
  897.3 6.6 all-to-all-done.13
  904.0 33.5 %all-reduce.6 = f32[4736]{0:T(1024)S(1)} all-reduce(f32[4736]{0:T(1024)S(1)} %subtract_dynamic-update-slice_fusion.1), channel_id=1, replica_groups=mesh['row'=4,'col'=8] {'col'}, use_global_device_ids=true, to_apply=%add.6 | all-reduce | flops 4736 | bytes 37888
  937.5 14.8 %add_reduce_fusion = f32[2368]{0:T(1024)S(1)} fusion(f32[2368,4736]{1,0:T(8,128)} %get-tuple-element.3, f32[4736]{0:T(1024)S(1)} %all-reduce.6), kind=kLoop, calls=%fused_computation.9 | loop fusion | flops 22427328 | bytes 44887808 | tf_op jit(solution)/shard_map/reduce_max | solution.py:30
  956.2 15.9 %exponential_reduce_fusion = f32[2368]{0:T(1024)S(1)} fusion(f32[2368,4736]{1,0:T(8,128)} %get-tuple-element.3, f32[2368]{0:T(1024)S(1)} %add_reduce_fusion, f32[4736]{0:T(1024)S(1)} %all-reduce.6), kind=kLoop, calls=%fused_computation | loop fusion | flops 33642176 | bytes 44897280 | tf_op jit(solution)/shard_map/reduce_sum | solution.py:31
  976.1 3.8 all-to-all-done.15
  980.0 10.7 %all-reduce.7 = f32[2368]{0:T(1024)} all-reduce(f32[2368]{0:T(1024)S(1)} %subtract_dynamic-update-slice_fusion), channel_id=1, replica_groups=mesh['row'=4,'col'=8] {'row'}, use_global_device_ids=true, to_apply=%add.7 | all-reduce | flops 2368 | bytes 18944
  (85 shorter events, 56.9 us)
Async XLA Ops:
  7.2 377.3 %all-gather.2.cloned.1.call-start = ((), (), s32[]{:S(2)}) async-start(), calls=%async_computation.16 | async-start | bytes 21823488 | tf_op jit(solution)/shard_map/all_gather | solution.py:57
  7.9 29.9 %collective-permute-start = (bf16[512,2368]{0,1:T(8,128)(2,1)}, bf16[512,2368]{0,1:T(8,128)(2,1)S(1)}, u32[]{:S(2)}, u32[]{:S(2)}) collective-permute-start(bf16[512,2368]{0,1:T(8,128)(2,1)} %param.3), channel_id=1, source_target_pairs={{0,8},{8,16},{16,24},{24,0},{1,9},{9,17},{17,25},{25,1},{2,10},{10... | collective-permute-start | bytes 7274504 | tf_op jit(solution)/shard_map/ppermute | solution.py:49
  37.8 29.1 %collective-permute-start.1 = (bf16[512,2368]{0,1:T(8,128)(2,1)S(1)}, bf16[512,2368]{0,1:T(8,128)(2,1)}, u32[]{:S(2)}, u32[]{:S(2)}) collective-permute-start(bf16[512,2368]{0,1:T(8,128)(2,1)S(1)} %collective-permute-done), channel_id=1, source_target_pairs={{0,8},{8,16},{16,24},{24,0},{1,9},{9,17},{17,25},{25,1},{2,10},{10... | collective-permute-start | bytes 7274504 | tf_op jit(solution)/shard_map/ppermute | solution.py:49
  66.9 29.3 %collective-permute-start.2 = (bf16[512,2368]{0,1:T(8,128)(2,1)}, bf16[512,2368]{0,1:T(8,128)(2,1)}, u32[]{:S(2)}, u32[]{:S(2)}) collective-permute-start(bf16[512,2368]{0,1:T(8,128)(2,1)} %collective-permute-done.1), channel_id=1, source_target_pairs={{0,8},{8,16},{16,24},{24,0},{1,9},{9,17},{17,25},{25,1},{2,10},{10... | collective-permute-start | bytes 7274504 | tf_op jit(solution)/shard_map/ppermute | solution.py:49
  452.6 29.3 %copy-start.2 = (u32[32]{0:T(128)S(1)}, u32[32]{0:T(128)}, u32[]{:S(2)}) copy-start(u32[32]{0:T(128)} %constant.51) | copy-start | bytes 388
  453.3 22.6 %all-to-all-start = ((f32[8,1,592]{2,1,0:T(1,128)}), f32[8,1,592]{2,1,0:T(1,128)S(1)}, u32[]{:S(2)}, u32[]{:S(2)}) async-start(f32[8,1,592]{2,1,0:T(1,128)} %all_to_all.128), calls=%async_computation | async-start | bytes 40960 | tf_op jit(solution)/shard_map/all_to_all | solution.py:18
  476.0 12.6 %all-to-all-start.1 = ((f32[8,1,592]{2,1,0:T(1,128)}), f32[8,1,592]{2,1,0:T(1,128)S(1)}, u32[]{:S(2)}, u32[]{:S(2)}) async-start(f32[8,1,592]{2,1,0:T(1,128)} %all_to_all.130), calls=%async_computation.1 | async-start | bytes 40960 | tf_op jit(solution)/shard_map/all_to_all | solution.py:21
  522.2 38.8 %copy-start.1 = (u32[32]{0:T(128)S(1)}, u32[32]{0:T(128)}, u32[]{:S(2)}) copy-start(u32[32]{0:T(128)} %constant.56) | copy-start | bytes 388
  537.7 20.0 %all-to-all-start.2 = ((f32[4,1,592]{2,1,0:T(1,128)}), f32[4,1,592]{2,1,0:T(1,128)S(1)}, u32[]{:S(2)}, u32[]{:S(2)}) async-start(f32[4,1,592]{2,1,0:T(1,128)} %all_to_all.134), calls=%async_computation.2 | async-start | bytes 20480 | tf_op jit(solution)/shard_map/all_to_all | solution.py:34
  557.7 7.0 all-to-all-start.3
  592.2 22.5 %all-to-all-start.4 = ((f32[8,1,592]{2,1,0:T(1,128)}), f32[8,1,592]{2,1,0:T(1,128)S(1)}, u32[]{:S(2)}, u32[]{:S(2)}) async-start(f32[8,1,592]{2,1,0:T(1,128)} %all_to_all.140), calls=%async_computation.4 | async-start | bytes 40960 | tf_op jit(solution)/shard_map/all_to_all | solution.py:18
  614.6 12.5 %all-to-all-start.5 = ((f32[8,1,592]{2,1,0:T(1,128)}), f32[8,1,592]{2,1,0:T(1,128)S(1)}, u32[]{:S(2)}, u32[]{:S(2)}) async-start(f32[8,1,592]{2,1,0:T(1,128)} %all_to_all.142), calls=%async_computation.5 | async-start | bytes 40960 | tf_op jit(solution)/shard_map/all_to_all | solution.py:21
  676.2 19.8 %all-to-all-start.6 = ((f32[4,1,592]{2,1,0:T(1,128)}), f32[4,1,592]{2,1,0:T(1,128)S(1)}, u32[]{:S(2)}, u32[]{:S(2)}) async-start(f32[4,1,592]{2,1,0:T(1,128)} %all_to_all.146), calls=%async_computation.6 | async-start | bytes 20480 | tf_op jit(solution)/shard_map/all_to_all | solution.py:34
  696.0 7.1 all-to-all-start.7
  730.5 22.5 %all-to-all-start.8 = ((f32[8,1,592]{2,1,0:T(1,128)}), f32[8,1,592]{2,1,0:T(1,128)S(1)}, u32[]{:S(2)}, u32[]{:S(2)}) async-start(f32[8,1,592]{2,1,0:T(1,128)} %all_to_all.152), calls=%async_computation.8 | async-start | bytes 40960 | tf_op jit(solution)/shard_map/all_to_all | solution.py:18
  753.0 12.5 %all-to-all-start.9 = ((f32[8,1,592]{2,1,0:T(1,128)}), f32[8,1,592]{2,1,0:T(1,128)S(1)}, u32[]{:S(2)}, u32[]{:S(2)}) async-start(f32[8,1,592]{2,1,0:T(1,128)} %all_to_all.154), calls=%async_computation.9 | async-start | bytes 40960 | tf_op jit(solution)/shard_map/all_to_all | solution.py:21
  814.6 19.8 %all-to-all-start.10 = ((f32[4,1,592]{2,1,0:T(1,128)}), f32[4,1,592]{2,1,0:T(1,128)S(1)}, u32[]{:S(2)}, u32[]{:S(2)}) async-start(f32[4,1,592]{2,1,0:T(1,128)} %all_to_all.158), calls=%async_computation.10 | async-start | bytes 20480 | tf_op jit(solution)/shard_map/all_to_all | solution.py:34
  834.4 7.1 all-to-all-start.11
  868.9 22.7 %all-to-all-start.12 = ((f32[8,1,592]{2,1,0:T(1,128)}), f32[8,1,592]{2,1,0:T(1,128)S(1)}, u32[]{:S(2)}, u32[]{:S(2)}) async-start(f32[8,1,592]{2,1,0:T(1,128)} %all_to_all.164), calls=%async_computation.12 | async-start | bytes 40960 | tf_op jit(solution)/shard_map/all_to_all | solution.py:18
  891.6 12.3 %all-to-all-start.13 = ((f32[8,1,592]{2,1,0:T(1,128)}), f32[8,1,592]{2,1,0:T(1,128)S(1)}, u32[]{:S(2)}, u32[]{:S(2)}) async-start(f32[8,1,592]{2,1,0:T(1,128)} %all_to_all.166), calls=%async_computation.13 | async-start | bytes 40960 | tf_op jit(solution)/shard_map/all_to_all | solution.py:21
  937.5 34.6 %copy-start = (f32[4736]{0:T(1024)}, f32[4736]{0:T(1024)S(1)}, u32[]{:S(2)}) copy-start(f32[4736]{0:T(1024)S(1)} %all-reduce.6) | copy-start | bytes 56836
  953.0 19.8 %all-to-all-start.14 = ((f32[4,1,592]{2,1,0:T(1,128)}), f32[4,1,592]{2,1,0:T(1,128)S(1)}, u32[]{:S(2)}, u32[]{:S(2)}) async-start(f32[4,1,592]{2,1,0:T(1,128)} %all_to_all.170), calls=%async_computation.14 | async-start | bytes 20480 | tf_op jit(solution)/shard_map/all_to_all | solution.py:34
  972.8 7.1 all-to-all-start.15
Sparse Core Ops, SparseCore 0:
  9.5 374.9 all-gather.1
